TPU v7x, 32 devices: a 4x4x1 block of a 4x4x8 slice. The times are simulated.
32 devices in a mesh: dp: 2 (over z, core), tp: 16 (over x, y).
Axes of the slice: x: 4, y: 4, z: 1, core: 2. Of those that a mesh axis runs over, the one named last changes fastest.
The devices are a block of a 4x4x8 slice.
Arguments:
- x: bfloat16 [4096, 8192], P(('dp', 'tp')), parts along dimension 0
- dy: bfloat16 [4096, 8192], P(('dp', 'tp')), parts along dimension 0
- gate: bfloat16 [4096, 24576], P('dp', 'tp'), parts along dimension 0
- up: bfloat16 [4096, 24576], P('dp', 'tp'), parts along dimension 0
- w_gate: bfloat16 [8192, 24576], P(None, 'tp')
- w_up: bfloat16 [8192, 24576], P(None, 'tp')
- w_down: bfloat16 [24576, 8192], P('tp')
Outputs:
- output 1: bfloat16 [4096, 8192], P(('dp', 'tp')), parts along dimension 0
- output 2: bfloat16 [16384, 24576], P('dp', 'tp'), parts along dimension 0
- output 3: bfloat16 [16384, 24576], P('dp', 'tp'), parts along dimension 0
- output 4: bfloat16 [49152, 8192], P(('dp', 'tp')), parts along dimension 0
There are 2 independent parts. A program takes and returns all parts, laid end to end along the dimension named above; an argument that names none is the same for every part.
All inputs are finite; a program needn't handle non-finite values.
Results may differ from a plain program's by a relative error of at most 0.012.
Values are sent between devices in bfloat16 or wider.
A program may use at most 768 MiB of HBM per device.

v0:
```python
import jax
import jax.numpy as jnp


def act(gate, up):
    return jax.nn.silu(gate) * up


def solution(mesh):
    def step(x, dy, gate, up, w_gate, w_up, w_down):
        hidden, back = jax.vjp(act, gate.astype(jnp.float32), up.astype(jnp.float32))
        d_hidden = jnp.dot(dy, w_down.T, preferred_element_type=jnp.float32)
        d_gate, d_up = (g.astype(jnp.bfloat16) for g in back(d_hidden))
        dx = jnp.dot(d_gate, w_gate.T) + jnp.dot(d_up, w_up.T)
        groups = mesh.shape["dp"]

        def by_group(a, b):
            a, b = (t.reshape(groups, -1, t.shape[-1]) for t in (a, b))
            product = jnp.einsum("gta,gtb->gab", a, b, preferred_element_type=jnp.float32)
            return product.astype(jnp.bfloat16).reshape(-1, b.shape[-1])

        return dx, by_group(x, d_gate), by_group(x, d_up), by_group(hidden.astype(jnp.bfloat16), dy)

    return step
```

profile of v0, /device:TPU:97, one launch (start us, length us, event | category | flops | bytes accessed | tf_op | source)
XLA Modules:
  0.0 686.9 jit_solution(12776124521417456838)
XLA Ops:
  7.2 0.1 all-gather.11.cloned.1.call-start
  7.2 0.7 all-gather.11.cloned.1.call-update
  8.0 0.1 all-gather.13.cloned.1.call-start
  8.0 0.7 all-gather.13.cloned.1.call-update
  8.8 0.1 reduce-scatter.4.cloned.1.call-start
  8.9 196.6 %all-gather.11.cloned.1.call-done = bf16[2048,8192]{1,0:T(8,128)(2,1)} async-done(((bf16[128,8192]{1,0:T(8,128)(2,1)}), bf16[2048,8192]{1,0:T(8,128)(2,1)}) %all-gather.11.cloned.1.call-update) | async-done | bytes 33554448 | tf_op args[1]
  205.5 68.1 %fusion.8 = (bf16[2048,1536]{1,0:T(8,128)(2,1)}, f32[2048,1536]{1,0:T(8,128)}) fusion(bf16[2048,1536]{1,0:T(8,128)(2,1)} %param.3, bf16[2048,1536]{1,0:T(8,128)(2,1)} %param.2, bf16[2048,8192]{1,0:T(8,128)(2,1)} %all-gather.11.cloned.1.call-done, bf16[1536,8192]{1,0:T(8,128)(2,1)} %param.1), kind=kOutput, calls=%fused_computation.18 | convolution fusion | flops 51580502016 | bytes 90177536 | tf_op jit(solution)/dot_general | solution.py:12
  273.6 60.3 %fusion.11 = bf16[2048,8192]{1,0:T(8,128)(2,1)} fusion(bf16[2048,1536]{1,0:T(8,128)(2,1)} %get-tuple-element.4, bf16[8192,1536]{1,0:T(8,128)(2,1)} %param.4), kind=kOutput, calls=%fused_computation.21 | convolution fusion | flops 51539607552 | bytes 65011712 | tf_op jit(solution)/dot_general | solution.py:14
  333.9 73.1 %convolution_add_fusion = bf16[2048,8192]{1,0:T(8,128)(2,1)} fusion(bf16[2048,8192]{1,0:T(8,128)(2,1)} %fusion.11, bf16[8192,1536]{1,0:T(8,128)(2,1)} %param.5, f32[2048,1536]{1,0:T(8,128)} %get-tuple-element.5, bf16[2048,1536]{1,0:T(8,128)(2,1)} %param.3), kind=kOutput, calls=%fused_computation.5 | convolution fusion | flops 51578404864 | bytes 111149056 | tf_op jit(solution)/dot_general | solution.py:14
  406.9 0.1 reduce-scatter.4.cloned.1.call-update
  407.0 0.0 all-gather.13.cloned.1.call-done
  407.0 71.9 %fusion.1 = bf16[8192,1536]{0,1:T(8,128)(2,1)} fusion(bf16[2048,8192]{1,0:T(8,128)(2,1)} %all-gather.13.cloned.1.call-done, f32[2048,1536]{1,0:T(8,128)} %get-tuple-element.5, bf16[2048,1536]{1,0:T(8,128)(2,1)} %param.3), kind=kOutput, calls=%fused_computation.4 | convolution fusion | flops 51574210560 | bytes 77594624 | tf_op jit(solution)/gta,gtb->gab/dot_general | solution.py:19
  478.9 32.6 %copy.1 = bf16[8192,1536]{1,0:T(8,128)(2,1)} copy(bf16[8192,1536]{0,1:T(8,128)(2,1)} %fusion.1) | data formatting | bytes 50331648
  511.5 60.0 %fusion = bf16[8192,1536]{0,1:T(8,128)(2,1)} fusion(bf16[2048,1536]{1,0:T(8,128)(2,1)} %get-tuple-element.4, bf16[2048,8192]{1,0:T(8,128)(2,1)} %all-gather.13.cloned.1.call-done), kind=kOutput, calls=%fused_computation.3 | convolution fusion | flops 51552190464 | bytes 65011712 | tf_op jit(solution)/gta,gtb->gab/dot_general | solution.py:19
  571.5 32.6 %copy = bf16[8192,1536]{1,0:T(8,128)(2,1)} copy(bf16[8192,1536]{0,1:T(8,128)(2,1)} %fusion) | data formatting | bytes 50331648
  604.0 75.8 %convolution_convert_fusion = bf16[1536,8192]{1,0:T(8,128)(2,1)} fusion(bf16[2048,8192]{1,0:T(8,128)(2,1)} %all-gather.11.cloned.1.call-done, bf16[2048,1536]{1,0:T(8,128)(2,1)} %param.2, bf16[2048,1536]{1,0:T(8,128)(2,1)} %param.3), kind=kOutput, calls=%fused_computation | convolution fusion | flops 51577356288 | bytes 71303168 | tf_op jit(solution)/gta,gtb->gab/dot_general | solution.py:19
  679.9 0.0 reduce-scatter.4.cloned.1.call-done
Async XLA Ops:
  7.2 198.3 %all-gather.11.cloned.1.call-start = ((), (), s32[]{:S(2)}) async-start(), calls=%async_computation.1 | async-start | bytes 35651584 | tf_op args[1]
  8.0 399.0 %all-gather.13.cloned.1.call-start = ((), (), s32[]{:S(2)}) async-start(), calls=%async_computation.2 | async-start | bytes 35651584 | tf_op jit(solution)/reshape | solution.py:18
  8.8 671.1 %reduce-scatter.4.cloned.1.call-start = ((), (), s32[]{:S(2)}) async-start(), calls=%async_computation.3 | async-start | bytes 35651584
Sparse Core Ops, SparseCore 0:
  10.0 195.4 all-gather.10
  207.4 191.4 all-gather.12
  407.1 189.1 reduce-scatter.3
where the time goes:
time: 694 us; the launch traced here: 687 us
  matrix products  409 us (59%)
  waiting for transfers between devices  198 us (29%)
  local copies, waits for them, and re-layouts  65.1 us (9%)
  between operations  14.3 us (2%)
    dot_general x3, matrix products, by_group(): jnp.einsum('gta,gtb->gab', a, b, preferred_element_type=jnp.float32)  208 us
    unnamed x5, waiting for transfers between devices  198 us
    dot_general x2, matrix products, step(): dx = jnp.dot(d_gate, w_gate.T) + jnp.dot(d_up, w_up.T)  133 us
    dot_general x1, matrix products, step(): d_hidden = jnp.dot(dy, w_down.T, preferred_element_type=jnp.float32)  68.1 us
    unnamed x2, local copies, waits for them, and re-layouts  65.1 us
  transfers between devices with their start and end apart: 3, of which 1 were waited for; matrix products, arithmetic and copies ran while one was open for 69% of the time, Pallas kernels for 0%

commit v1 on v0

v1 whole, which is shorter than its diff:
```python
import functools
import math

import jax
import jax.numpy as jnp
from jax import lax
from jax.experimental import pallas as pl
from jax.experimental.pallas import tpu as pltpu
from jax.sharding import PartitionSpec as P

RINGS = 4
SUBS = 4
BF16 = jnp.bfloat16
F32 = jnp.float32
NT = (((1,), (1,)), ((), ()))
TN = (((0,), (0,)), ((), ()))


def act_grads(g, u, dh):
    sig = jax.nn.sigmoid(g)
    silu = g * sig
    ds = dh * u
    return silu * u, ds * (sig + silu * (1.0 - sig)), dh * silu


def gather_kernel(
    n, tile_f, tile_d,
    x_ref, dy_ref, gate_ref, up_ref, wg_ref, wu_ref, wd_ref,
    full_ref, dg_ref, du_ref, hid_ref, dx_ref,
    blk, wd_buf, w2_buf, gu_buf, dh_buf, grads, obuf,
    send_sem, recv_sem, blk_sem, wd_sem, w2_sem, gu_sem, grads_sem, o_sem,
):
    side = math.isqrt(n)
    rows, d_model = x_ref.shape
    ff = gate_ref.shape[1]
    piece = rows // RINGS
    sub_rows = piece // SUBS
    hops = n - 1
    per_block = blk.shape[0] // rows
    blocks = n // per_block
    tiles_a = ff // tile_f
    tiles_b = d_model // tile_d
    tiles = tiles_a + tiles_b
    messages = 2 * hops * SUBS

    me = lax.axis_index("tp")
    a, b = me // side, me % side
    place = (a * side + (a + b) % side, b * side + (a + b) % side)

    def device(ring, k):
        k = (k + 2 * n) % n
        u = k // side
        v = (k - u) % side
        return u * side + v if ring // 2 == 0 else v * side + u

    def owner(ring, distance):
        return device(ring, place[ring // 2] - distance if ring % 2 == 0 else place[ring // 2] + distance)

    def following(ring):
        return owner(ring, -1)

    def rows_of(ring, distance):
        return pl.multiple_of(owner(ring, distance) * rows + ring * piece, piece)

    barrier = pltpu.get_barrier_semaphore()
    for ring in range(RINGS):
        pl.semaphore_signal(barrier, inc=1, device_id={"tp": following(ring)}, device_id_type=pl.DeviceIdType.MESH)
    pl.semaphore_wait(barrier, RINGS)

    def message(ring, src, which, distance, sub, index):
        start = pl.multiple_of(rows_of(ring, distance) + sub * sub_rows, sub_rows)
        there = full_ref.at[which, pl.ds(start, sub_rows), :]
        return pltpu.make_async_remote_copy(
            src_ref=there if src is None else src,
            dst_ref=there,
            send_sem=send_sem,
            recv_sem=recv_sem.at[ring, index],
            device_id={"tp": following(ring)},
            device_id_type=pl.DeviceIdType.MESH,
        )

    for sub in range(SUBS):
        for ring in range(RINGS):
            own = dy_ref.at[pl.ds(ring * piece + sub * sub_rows, sub_rows), :]
            message(ring, own, 0, 0, sub, sub).start()

    mine = pl.ds(pl.multiple_of(me * rows, rows), rows)
    bounce = [blk.at[pl.ds(i * rows, rows), :] for i in range(2)]
    for i, ref in enumerate((dy_ref, x_ref)):
        pltpu.make_async_copy(ref, bounce[i], wd_sem.at[i]).start()
    for i, ref in enumerate((dy_ref, x_ref)):
        pltpu.make_async_copy(ref, bounce[i], wd_sem.at[i]).wait()
        pltpu.make_async_copy(bounce[i], full_ref.at[i, mine, :], wd_sem.at[i]).start()
    for i in range(2):
        pltpu.make_async_copy(bounce[i], full_ref.at[i, mine, :], wd_sem.at[i]).wait()

    def serve(index, carry=None):
        step, sub = index // SUBS + 1, index % SUBS
        for ring in range(RINGS):
            message(ring, None, (step - 1) // hops, (step - 1) % hops + 1, sub, index).wait_recv()

        @pl.when(step < 2 * hops)
        def _():
            for ring in range(RINGS):
                message(ring, None, step // hops, step % hops, sub, index + SUBS).start()

    def served_before(tile):
        first = (per_block - 1) * SUBS
        return first + tile * (messages - first) // (blocks * tiles)

    def serve_after(tile):
        lax.fori_loop(served_before(tile), served_before(tile + 1), lambda i, c: serve(i), None)

    def load_wd(j, slot):
        src = wd_ref.at[pl.ds(pl.multiple_of(j * tile_f, tile_f), tile_f), :]
        return pltpu.make_async_copy(src, wd_buf.at[slot], wd_sem.at[slot])

    def load_w2(j, slot):
        at = pl.ds(pl.multiple_of(j * tile_d, tile_d), tile_d)
        return [
            pltpu.make_async_copy(ref.at[at, :], w2_buf.at[slot, i], w2_sem.at[slot, i])
            for i, ref in enumerate((wg_ref, wu_ref))
        ]

    def pieces(block, body):
        def by_distance(i, carry):
            for ring in range(RINGS):
                body(
                    rows_of(ring, block * per_block + i),
                    pl.multiple_of(i * rows + ring * piece, piece),
                )

        lax.fori_loop(0, per_block, by_distance, None)

    load_wd(0, 0).start()
    lax.fori_loop(0, (per_block - 1) * SUBS, lambda i, c: serve(i), None)

    def one_block(block, carry):
        for c in load_w2(0, 0):
            c.start()

        def fetch(there, here):
            pltpu.make_async_copy(full_ref.at[0, pl.ds(there, piece), :], blk.at[pl.ds(here, piece), :], blk_sem).start()
            for i, ref in enumerate((gate_ref, up_ref)):
                pltpu.make_async_copy(
                    ref.at[pl.ds(there, piece), :], gu_buf.at[i, pl.ds(here, piece), :], gu_sem.at[i]
                ).start()

        pieces(block, fetch)
        pltpu.make_async_copy(full_ref.at[0, pl.ds(0, blk.shape[0]), :], blk, blk_sem).wait()
        for i, ref in enumerate((gate_ref, up_ref)):
            pltpu.make_async_copy(ref.at[pl.ds(0, blk.shape[0]), :], gu_buf.at[i], gu_sem.at[i]).wait()

        def tile_a_body(j, carry):
            slot = j % 2
            load_wd(j, slot).wait()

            @pl.when(j + 1 < tiles_a)
            def _():
                load_wd(j + 1, 1 - slot).start()

            dh_buf[...] = lax.dot_general(blk[...], wd_buf[slot], NT, preferred_element_type=F32)
            cols = pl.ds(pl.multiple_of(j * tile_f, tile_f), tile_f)
            chunk = 32

            def elementwise(i, c):
                at = pl.ds(pl.multiple_of(i * chunk, chunk), chunk)
                h, dgate, dup = act_grads(
                    gu_buf[0, at, cols].astype(F32), gu_buf[1, at, cols].astype(F32), dh_buf[at, :]
                )
                grads[0, at, cols] = dgate.astype(BF16)
                grads[1, at, cols] = dup.astype(BF16)
                grads[2, at, cols] = h.astype(BF16)

            lax.fori_loop(0, blk.shape[0] // chunk, elementwise, None)
            serve_after(block * tiles + j)

        lax.fori_loop(0, tiles_a, tile_a_body, None)

        def put_grads(there, here):
            for i, ref in enumerate((dg_ref, du_ref, hid_ref)):
                pltpu.make_async_copy(
                    grads.at[i, pl.ds(here, piece), :], ref.at[pl.ds(there, piece), :], grads_sem.at[i]
                ).start()

        pieces(block, put_grads)

        @pl.when(block + 1 < blocks)
        def _():
            load_wd(0, 0).start()

        def wait_out(slot):
            pltpu.make_async_copy(
                obuf.at[slot], dx_ref.at[pl.ds(0, blk.shape[0]), pl.ds(0, tile_d)], o_sem.at[slot]
            ).wait()

        def tile_b_body(j, carry):
            slot = j % 2
            for c in load_w2(j, slot):
                c.wait()

            @pl.when(j + 1 < tiles_b)
            def _():
                for c in load_w2(j + 1, 1 - slot):
                    c.start()

            @pl.when(j >= 2)
            def _():
                wait_out(slot)

            obuf[slot] = (
                lax.dot_general(grads[0], w2_buf[slot, 0], NT, preferred_element_type=F32)
                + lax.dot_general(grads[1], w2_buf[slot, 1], NT, preferred_element_type=F32)
            ).astype(BF16)
            cols = pl.ds(pl.multiple_of(j * tile_d, tile_d), tile_d)

            def put(there, here):
                pltpu.make_async_copy(
                    obuf.at[slot, pl.ds(here, piece), :], dx_ref.at[pl.ds(there, piece), cols], o_sem.at[slot]
                ).start()

            pieces(block, put)
            serve_after(block * tiles + tiles_a + j)

        lax.fori_loop(0, tiles_b, tile_b_body, None)
        for slot in range(2):
            wait_out(slot)
        for i, ref in enumerate((dg_ref, du_ref, hid_ref)):
            pltpu.make_async_copy(grads.at[i], ref.at[pl.ds(0, blk.shape[0]), :], grads_sem.at[i]).wait()

    lax.fori_loop(0, blocks, one_block, None)
    sent = full_ref.at[:, pl.ds(0, hops * rows), :]
    pltpu.make_async_copy(sent, sent, send_sem).wait()


def gather(mesh, x, dy, gate, up, w_gate, w_up, w_down, tile_f=256, tile_d=512, block=512):
    n = mesh.shape["tp"]
    rows, d_model = x.shape
    total, ff = gate.shape
    tile_f, tile_d, block = min(tile_f, ff), min(tile_d, d_model), min(block, total)
    hbm = pl.BlockSpec(memory_space=pl.ANY)
    kept = jax.ShapeDtypeStruct((total, ff), BF16)
    messages = 2 * (n - 1) * SUBS
    return pl.pallas_call(
        functools.partial(gather_kernel, n, tile_f, tile_d),
        name="gather",
        out_shape=(
            jax.ShapeDtypeStruct((2, total, d_model), BF16),
            kept, kept, kept,
            jax.ShapeDtypeStruct((total, d_model), BF16),
        ),
        in_specs=[hbm] * 7,
        out_specs=(hbm,) * 5,
        scratch_shapes=[
            pltpu.VMEM((block, d_model), BF16),
            pltpu.VMEM((2, tile_f, d_model), BF16),
            pltpu.VMEM((2, 2, tile_d, ff), BF16),
            pltpu.VMEM((2, block, ff), BF16),
            pltpu.VMEM((block, tile_f), F32),
            pltpu.VMEM((3, block, ff), BF16),
            pltpu.VMEM((2, block, tile_d), BF16),
            pltpu.SemaphoreType.DMA,
            pltpu.SemaphoreType.DMA((RINGS, messages)),
            pltpu.SemaphoreType.DMA,
            pltpu.SemaphoreType.DMA((2,)),
            pltpu.SemaphoreType.DMA((2, 2)),
            pltpu.SemaphoreType.DMA((2,)),
            pltpu.SemaphoreType.DMA((3,)),
            pltpu.SemaphoreType.DMA((2,)),
        ],
        compiler_params=pltpu.CompilerParams(collective_id=0, has_side_effects=True, vmem_limit_bytes=58 * 2**20),
        cost_estimate=pl.CostEstimate(
            flops=6 * total * d_model * ff, bytes_accessed=2 * 4 * 3 * ff * d_model, transcendentals=total * ff
        ),
    )(x, dy, gate, up, w_gate, w_up, w_down)


def solution(mesh):
    rows = P(("dp", "tp"), None)
    both = P("dp", "tp")
    cols = P(None, "tp")

    def body(x, dy, gate, up, w_gate, w_up, w_down):
        full, d_gate, d_up, hidden, dx = gather(mesh, x, dy, gate, up, w_gate, w_up, w_down)
        dx = lax.psum_scatter(dx, "tp", scatter_dimension=0, tiled=True)

        def dw(a, b):
            return lax.dot_general(a, b, TN, preferred_element_type=F32).astype(BF16)

        return dx, dw(full[1], d_gate), dw(full[1], d_up), dw(hidden, full[0])

    return jax.shard_map(
        body,
        mesh=mesh,
        in_specs=(rows, rows, both, both, cols, cols, P("tp", None)),
        out_specs=(rows, both, both, rows),
        check_vma=False,
    )
```

time: 694 us -> 553 us (0.80); the launches traced: 687 us -> 553 us
  Pallas kernels: 0 us -> 348 us
  matrix products: 409 us -> 179 us
  waiting for transfers between devices: 198 us -> 11.5 us
  local copies, waits for them, and re-layouts: 65.1 us -> 0.02 us
    pallas_call x0 -> x1, Pallas kernels: none -> 348 us  [gather(): pl.pallas_call(functools.partial(gather_kernel, n, tile_f, tile_d), name=...]
    dot_general x6 -> x3, matrix products: 409 us -> 179 us  [dw(): return lax.dot_general(a, b, TN, preferred_element_type=F32).astype(BF16)]
    unnamed x5 -> x1, waiting for transfers between devices: 198 us -> 0.05 us
    unnamed x2 -> x8, local copies, waits for them, and re-layouts: 65.1 us -> 0.02 us
    reduce_scatter x0 -> x1, waiting for transfers between devices: none -> 11.5 us  [body(): dx = lax.psum_scatter(dx, 'tp', scatter_dimension=0, tiled=True)]
  transfers between devices with their start and end apart: 3 -> 1, of which waited for: 1 -> 1; matrix products, arithmetic and copies ran while one was open for 69% -> 32% of each run, Pallas kernels for 0% -> 0%
where the time goes in v1:
time: 553 us
  Pallas kernels  348 us (63%)
  matrix products  179 us (32%)
  between operations  14.1 us (3%)
  waiting for transfers between devices  11.5 us (2%)
    pallas_call x1, Pallas kernels, gather(): pl.pallas_call(functools.partial(gather_kernel, n, tile_f, tile_d), name=...  348 us
    dot_general x3, matrix products, dw(): return lax.dot_general(a, b, TN, preferred_element_type=F32).astype(BF16)  179 us
    reduce_scatter x1, waiting for transfers between devices, body(): dx = lax.psum_scatter(dx, 'tp', scatter_dimension=0, tiled=True)  11.5 us
  transfers between devices with their start and end apart: 1, of which 1 were waited for; matrix products, arithmetic and copies ran while one was open for 32% of the time, Pallas kernels for 0%

profile of v1, /device:TPU:97, one launch (start us, length us, event | category | flops | bytes accessed | tf_op | source)
XLA Modules:
  0.0 553.1 jit_solution(14012589792990336830)
XLA Ops:
  7.2 0.1 reduce-scatter.2.cloned.1.call-start
  7.2 348.4 %gather.1 = (bf16[2,2048,8192]{2,1,0:T(8,128)(2,1)}, bf16[2048,1536]{1,0:T(8,128)(2,1)}, bf16[2048,1536]{1,0:T(8,128)(2,1)}, bf16[2048,1536]{1,0:T(8,128)(2,1)}, bf16[2048,8192]{1,0:T(8,128)(2,1)}) custom-call(bf16[128,8192]{1,0:T(8,128)(2,1)} %x_ref.1, bf16[128,8192]{1,0:T(8,128)(2,1)} %dy_ref.1, bf16[2048,1536]{1,0:T(8,128)(2,1)} %gate_ref.1, ...), custom_call_target="tpu_custom_call" | custom-call | flops 154618822656 | bytes 301989888 | tf_op jit(solution)/shard_map/gather/pallas_call | solution.py:244
  355.6 0.0 slice-start.2
  355.6 0.1 reduce-scatter.2.cloned.1.call-update
  355.7 0.0 slice-start.3
  355.7 0.0 slice-start
  355.7 60.2 %fusion.7 = bf16[8192,1536]{1,0:T(8,128)(2,1)} fusion(bf16[2048,1536]{1,0:T(8,128)(2,1)} %get-tuple-element.11, bf16[2,2048,8192]{2,1,0:T(8,128)(2,1)} %get-tuple-element.10), kind=kOutput, calls=%fused_computation.7 | convolution fusion | flops 51552190464 | bytes 65011712 | tf_op jit(solution)/shard_map/dot_general | solution.py:288
  415.9 0.0 slice-done.2
  415.9 0.0 slice-done.3
  416.0 0.0 slice-start.1
  416.0 58.5 %fusion.10 = bf16[8192,1536]{1,0:T(8,128)(2,1)} fusion(bf16[2048,1536]{1,0:T(8,128)(2,1)S(1)} %bitcast.26, bf16[2,2048,8192]{2,1,0:T(8,128)(2,1)} %get-tuple-element.10), kind=kOutput, calls=%fused_computation.8 | convolution fusion | flops 51552190464 | bytes 65011712 | tf_op jit(solution)/shard_map/dot_general | solution.py:288
  474.5 0.0 slice-done
  474.5 0.0 slice-done.1
  474.5 60.3 %fusion.13 = bf16[1536,8192]{1,0:T(8,128)(2,1)} fusion(bf16[2048,1536]{1,0:T(8,128)(2,1)S(1)} %bitcast.24, bf16[2,2048,8192]{2,1,0:T(8,128)(2,1)} %get-tuple-element.10), kind=kOutput, calls=%fused_computation.9 | convolution fusion | flops 51552190464 | bytes 65011712 | tf_op jit(solution)/shard_map/dot_general | solution.py:288
  534.8 11.5 %reduce-scatter.2.cloned.1.call-done = bf16[128,8192]{1,0:T(8,128)(2,1)} async-done(((bf16[2048,8192]{1,0:T(8,128)(2,1)}), bf16[128,8192]{1,0:T(8,128)(2,1)}) %reduce-scatter.2.cloned.1.call-update) | async-done | bytes 2097168 | tf_op jit(solution)/shard_map/reduce_scatter | solution.py:285
  (2 shorter events, 0.0 us)
Async XLA Ops:
  7.2 539.1 %reduce-scatter.2.cloned.1.call-start = ((), (), s32[]{:S(2)}) async-start(), calls=%async_computation.1 | async-start | bytes 35651584 | tf_op jit(solution)/shard_map/reduce_scatter | solution.py:285
  355.6 60.3 %slice-start.2 = ((s8[6291456]{0:T(1024)(128)(4,1)}), s8[2097152]{0:T(1024)(128)(4,1)S(1)}, s32[]{:S(2)}) async-start(s8[6291456]{0:T(1024)(128)(4,1)} %bitcast.25), calls=%async_computation.4 | async-start | bytes 4194304
  355.7 60.3 %slice-start.3 = ((s8[6291456]{0:T(1024)(128)(4,1)}), s8[4194304]{0:T(1024)(128)(4,1)S(1)}, s32[]{:S(2)}) async-start(s8[6291456]{0:T(1024)(128)(4,1)} %bitcast.25), calls=%async_computation.5 | async-start | bytes 8388608
  355.7 118.8 %slice-start = ((s8[6291456]{0:T(1024)(128)(4,1)}), s8[4194304]{0:T(1024)(128)(4,1)S(1)}, s32[]{:S(2)}) async-start(s8[6291456]{0:T(1024)(128)(4,1)} %bitcast.23), calls=%async_computation.2 | async-start | bytes 8388608
  416.0 58.5 %slice-start.1 = ((s8[6291456]{0:T(1024)(128)(4,1)}), s8[2097152]{0:T(1024)(128)(4,1)S(1)}, s32[]{:S(2)}) async-start(s8[6291456]{0:T(1024)(128)(4,1)} %bitcast.23), calls=%async_computation.3 | async-start | bytes 4194304
Sparse Core Ops, SparseCore 0:
  355.8 190.4 reduce-scatter.1

commit v2 on v1

--- a/solution.py
+++ b/solution.py
@@ -10,6 +10,9 @@
 
 RINGS = 4
 SUBS = 4
+LATE = 3
+FETCH = 2
+TILE_A = 2
 BF16 = jnp.bfloat16
 F32 = jnp.float32
 NT = (((1,), (1,)), ((), ()))
@@ -21,6 +24,75 @@
     silu = g * sig
     ds = dh * u
     return silu * u, ds * (sig + silu * (1.0 - sig)), dh * silu
+
+
+class Ring:
+    def __init__(self, n, rows, full_ref, send_sem, recv_sem):
+        self.n, self.rows, self.full_ref, self.send_sem, self.recv_sem = n, rows, full_ref, send_sem, recv_sem
+        self.side = math.isqrt(n)
+        self.hops = n - 1
+        self.piece = rows // RINGS
+        self.sub_rows = self.piece // SUBS
+        self.me = lax.axis_index("tp")
+        a, b = self.me // self.side, self.me % self.side
+        self.place = (a * self.side + (a + b) % self.side, b * self.side + (a + b) % self.side)
+
+    def owner(self, r, distance):
+        k = self.place[r // 2] - distance if r % 2 == 0 else self.place[r // 2] + distance
+        k = (k + 2 * self.n) % self.n
+        u = k // self.side
+        v = (k - u) % self.side
+        return u * self.side + v if r // 2 == 0 else v * self.side + u
+
+    def following(self, r):
+        return {"tp": self.owner(r, -1)}
+
+    def rows_of(self, r, distance):
+        return pl.multiple_of(self.owner(r, distance) * self.rows + r * self.piece, self.piece)
+
+    def greet(self):
+        barrier = pltpu.get_barrier_semaphore()
+        for r in range(RINGS):
+            pl.semaphore_signal(barrier, inc=1, device_id=self.following(r), device_id_type=pl.DeviceIdType.MESH)
+        pl.semaphore_wait(barrier, RINGS)
+
+    def message(self, r, step, sub, slot, src=None):
+        start = pl.multiple_of(self.rows_of(r, step % self.hops) + sub * self.sub_rows, self.sub_rows)
+        there = self.full_ref.at[step // self.hops, pl.ds(start, self.sub_rows), :]
+        return pltpu.make_async_remote_copy(
+            src_ref=there if src is None else src,
+            dst_ref=there,
+            send_sem=self.send_sem,
+            recv_sem=self.recv_sem.at[r, slot],
+            device_id=self.following(r),
+            device_id_type=pl.DeviceIdType.MESH,
+        )
+
+    def arrival(self, r, step, sub, slot):
+        start = pl.multiple_of(self.rows_of(r, (step - 1) % self.hops + 1) + sub * self.sub_rows, self.sub_rows)
+        there = self.full_ref.at[(step - 1) // self.hops, pl.ds(start, self.sub_rows), :]
+        return pltpu.make_async_remote_copy(
+            src_ref=there,
+            dst_ref=there,
+            send_sem=self.send_sem,
+            recv_sem=self.recv_sem.at[r, slot],
+            device_id=self.following(r),
+            device_id_type=pl.DeviceIdType.MESH,
+        )
+
+    def serve(self, index, slot, stop):
+        step, sub = index // SUBS + 1, index % SUBS
+        for r in range(RINGS):
+            self.arrival(r, step, sub, slot).wait_recv()
+
+        @pl.when(index + SUBS < stop)
+        def _():
+            for r in range(RINGS):
+                self.message(r, step, sub, slot + SUBS).start()
+
+    def sent(self, messages):
+        whole = self.full_ref.at[:, pl.ds(0, messages // SUBS * self.rows // 2), :]
+        pltpu.make_async_copy(whole, whole, self.send_sem).wait()
 
 
 def gather_kernel(
@@ -40,49 +112,17 @@
     blocks = n // per_block
     tiles_a = ff // tile_f
     tiles_b = d_model // tile_d
-    tiles = tiles_a + tiles_b
-    messages = 2 * hops * SUBS
-
-    me = lax.axis_index("tp")
-    a, b = me // side, me % side
-    place = (a * side + (a + b) % side, b * side + (a + b) % side)
-
-    def device(ring, k):
-        k = (k + 2 * n) % n
-        u = k // side
-        v = (k - u) % side
-        return u * side + v if ring // 2 == 0 else v * side + u
-
-    def owner(ring, distance):
-        return device(ring, place[ring // 2] - distance if ring % 2 == 0 else place[ring // 2] + distance)
-
-    def following(ring):
-        return owner(ring, -1)
-
-    def rows_of(ring, distance):
-        return pl.multiple_of(owner(ring, distance) * rows + ring * piece, piece)
-
-    barrier = pltpu.get_barrier_semaphore()
-    for ring in range(RINGS):
-        pl.semaphore_signal(barrier, inc=1, device_id={"tp": following(ring)}, device_id_type=pl.DeviceIdType.MESH)
-    pl.semaphore_wait(barrier, RINGS)
-
-    def message(ring, src, which, distance, sub, index):
-        start = pl.multiple_of(rows_of(ring, distance) + sub * sub_rows, sub_rows)
-        there = full_ref.at[which, pl.ds(start, sub_rows), :]
-        return pltpu.make_async_remote_copy(
-            src_ref=there if src is None else src,
-            dst_ref=there,
-            send_sem=send_sem,
-            recv_sem=recv_sem.at[ring, index],
-            device_id={"tp": following(ring)},
-            device_id_type=pl.DeviceIdType.MESH,
-        )
-
+    messages = (2 * hops - LATE) * SUBS
+
+    ring = Ring(n, x_ref.shape[0], full_ref, send_sem, recv_sem)
+    me = ring.me
+    rows_of = ring.rows_of
+
+    ring.greet()
     for sub in range(SUBS):
-        for ring in range(RINGS):
-            own = dy_ref.at[pl.ds(ring * piece + sub * sub_rows, sub_rows), :]
-            message(ring, own, 0, 0, sub, sub).start()
+        for r in range(RINGS):
+            own = dy_ref.at[pl.ds(r * piece + sub * sub_rows, sub_rows), :]
+            ring.message(r, 0, sub, sub, own).start()
 
     mine = pl.ds(pl.multiple_of(me * rows, rows), rows)
     bounce = [blk.at[pl.ds(i * rows, rows), :] for i in range(2)]
@@ -94,22 +134,17 @@
     for i in range(2):
         pltpu.make_async_copy(bounce[i], full_ref.at[i, mine, :], wd_sem.at[i]).wait()
 
-    def serve(index, carry=None):
-        step, sub = index // SUBS + 1, index % SUBS
-        for ring in range(RINGS):
-            message(ring, None, (step - 1) // hops, (step - 1) % hops + 1, sub, index).wait_recv()
-
-        @pl.when(step < 2 * hops)
-        def _():
-            for ring in range(RINGS):
-                message(ring, None, step // hops, step % hops, sub, index + SUBS).start()
-
-    def served_before(tile):
-        first = (per_block - 1) * SUBS
-        return first + tile * (messages - first) // (blocks * tiles)
-
-    def serve_after(tile):
-        lax.fori_loop(served_before(tile), served_before(tile + 1), lambda i, c: serve(i), None)
+    def serve(index):
+        ring.serve(index, index, messages)
+
+    units = FETCH + TILE_A * tiles_a + tiles_b
+    first = (per_block - 1) * SUBS
+
+    def serve_between(block, since, until):
+        def served(unit):
+            return first + (block * units + unit) * (messages - first) // (blocks * units)
+
+        lax.fori_loop(served(since), served(until), lambda i, c: serve(i), None)
 
     def load_wd(j, slot):
         src = wd_ref.at[pl.ds(pl.multiple_of(j * tile_f, tile_f), tile_f), :]
@@ -124,16 +159,16 @@
 
     def pieces(block, body):
         def by_distance(i, carry):
-            for ring in range(RINGS):
+            for r in range(RINGS):
                 body(
-                    rows_of(ring, block * per_block + i),
-                    pl.multiple_of(i * rows + ring * piece, piece),
+                    rows_of(r, block * per_block + i),
+                    pl.multiple_of(i * rows + r * piece, piece),
                 )
 
         lax.fori_loop(0, per_block, by_distance, None)
 
     load_wd(0, 0).start()
-    lax.fori_loop(0, (per_block - 1) * SUBS, lambda i, c: serve(i), None)
+    lax.fori_loop(0, first, lambda i, c: serve(i), None)
 
     def one_block(block, carry):
         for c in load_w2(0, 0):
@@ -147,6 +182,7 @@
                 ).start()
 
         pieces(block, fetch)
+        serve_between(block, 0, FETCH)
         pltpu.make_async_copy(full_ref.at[0, pl.ds(0, blk.shape[0]), :], blk, blk_sem).wait()
         for i, ref in enumerate((gate_ref, up_ref)):
             pltpu.make_async_copy(ref.at[pl.ds(0, blk.shape[0]), :], gu_buf.at[i], gu_sem.at[i]).wait()
@@ -173,7 +209,7 @@
                 grads[2, at, cols] = h.astype(BF16)
 
             lax.fori_loop(0, blk.shape[0] // chunk, elementwise, None)
-            serve_after(block * tiles + j)
+            serve_between(block, FETCH + TILE_A * j, FETCH + TILE_A * (j + 1))
 
         lax.fori_loop(0, tiles_a, tile_a_body, None)
 
@@ -220,7 +256,8 @@
                 ).start()
 
             pieces(block, put)
-            serve_after(block * tiles + tiles_a + j)
+            done = FETCH + TILE_A * tiles_a + j
+            serve_between(block, done, done + 1)
 
         lax.fori_loop(0, tiles_b, tile_b_body, None)
         for slot in range(2):
@@ -229,8 +266,7 @@
             pltpu.make_async_copy(grads.at[i], ref.at[pl.ds(0, blk.shape[0]), :], grads_sem.at[i]).wait()
 
     lax.fori_loop(0, blocks, one_block, None)
-    sent = full_ref.at[:, pl.ds(0, hops * rows), :]
-    pltpu.make_async_copy(sent, sent, send_sem).wait()
+    ring.sent(messages)
 
 
 def gather(mesh, x, dy, gate, up, w_gate, w_up, w_down, tile_f=256, tile_d=512, block=512):
@@ -240,7 +276,7 @@
     tile_f, tile_d, block = min(tile_f, ff), min(tile_d, d_model), min(block, total)
     hbm = pl.BlockSpec(memory_space=pl.ANY)
     kept = jax.ShapeDtypeStruct((total, ff), BF16)
-    messages = 2 * (n - 1) * SUBS
+    messages = (2 * (n - 1) - LATE) * SUBS
     return pl.pallas_call(
         functools.partial(gather_kernel, n, tile_f, tile_d),
         name="gather",
@@ -275,6 +311,114 @@
     )(x, dy, gate, up, w_gate, w_up, w_down)
 
 
+def late_kernel(
+    n, tile_d,
+    full_in_ref, hidden_ref,
+    full_ref, dw_ref,
+    hid, dy_buf, obuf,
+    send_sem, recv_sem, hid_sem, dy_sem, o_sem,
+):
+    del full_in_ref
+    total, d_model = full_ref.shape[1:]
+    ff = hidden_ref.shape[1]
+    tiles = d_model // tile_d
+    ring = Ring(n, total // n, full_ref, send_sem, recv_sem)
+    stop = 2 * ring.hops * SUBS
+    messages = LATE * SUBS
+    first = stop - messages
+
+    load = pltpu.make_async_copy(hidden_ref, hid, hid_sem)
+    load.start()
+
+    def load_dy(j, slot):
+        at = pl.ds(pl.multiple_of(j * tile_d, tile_d), tile_d)
+        return pltpu.make_async_copy(full_ref.at[0, :, at], dy_buf.at[slot], dy_sem.at[slot])
+
+    def store(j, slot):
+        at = pl.ds(pl.multiple_of(j * tile_d, tile_d), tile_d)
+        return pltpu.make_async_copy(obuf.at[slot], dw_ref.at[:, at], o_sem.at[slot])
+
+    load_dy(0, 0).start()
+    ring.greet()
+    for sub in range(SUBS):
+        for r in range(RINGS):
+            ring.message(r, first // SUBS, sub, sub).start()
+    load.wait()
+
+    def tile(j, carry):
+        slot = j % 2
+        load_dy(j, slot).wait()
+
+        @pl.when(j + 1 < tiles)
+        def _():
+            load_dy(j + 1, 1 - slot).start()
+
+        @pl.when(j >= 2)
+        def _():
+            store(j - 2, slot).wait()
+
+        obuf[slot] = lax.dot_general(hid[...], dy_buf[slot], TN, preferred_element_type=F32).astype(BF16)
+        store(j, slot).start()
+        lax.fori_loop(
+            j * messages // tiles,
+            (j + 1) * messages // tiles,
+            lambda i, c: ring.serve(first + i, i, stop),
+            None,
+        )
+
+    lax.fori_loop(0, tiles, tile, None)
+    for j in (tiles - 2, tiles - 1):
+        store(j, j % 2).wait()
+    ring.sent(messages)
+
+
+def finish(mesh, full, hidden, tile_d=256):
+    n = mesh.shape["tp"]
+    _, total, d_model = full.shape
+    ff = hidden.shape[1]
+    hbm = pl.BlockSpec(memory_space=pl.ANY)
+    return pl.pallas_call(
+        functools.partial(late_kernel, n, tile_d),
+        name="finish",
+        out_shape=(jax.ShapeDtypeStruct(full.shape, BF16), jax.ShapeDtypeStruct((ff, d_model), BF16)),
+        in_specs=[hbm] * 2,
+        out_specs=(hbm,) * 2,
+        input_output_aliases={0: 0},
+        scratch_shapes=[
+            pltpu.VMEM((total, ff), BF16),
+            pltpu.VMEM((2, total, tile_d), BF16),
+            pltpu.VMEM((2, ff, tile_d), BF16),
+            pltpu.SemaphoreType.DMA,
+            pltpu.SemaphoreType.DMA((RINGS, LATE * SUBS)),
+            pltpu.SemaphoreType.DMA,
+            pltpu.SemaphoreType.DMA((2,)),
+            pltpu.SemaphoreType.DMA((2,)),
+        ],
+        compiler_params=pltpu.CompilerParams(collective_id=1, has_side_effects=True, vmem_limit_bytes=60 * 2**20),
+        cost_estimate=pl.CostEstimate(
+            flops=2 * total * d_model * ff, bytes_accessed=2 * (total * ff + total * d_model + ff * d_model), transcendentals=0
+        ),
+    )(full, hidden)
+
+
+def copy_kernel(src_ref, out_ref):
+    out_ref[...] = src_ref[...]
+
+
+def copied(a, rows=256):
+    spec = pl.BlockSpec((rows, a.shape[1]), lambda i: (i, 0))
+    return pl.pallas_call(
+        copy_kernel,
+        name="copied",
+        grid=(a.shape[0] // rows,),
+        out_shape=jax.ShapeDtypeStruct(a.shape, a.dtype),
+        in_specs=[spec],
+        out_specs=spec,
+        compiler_params=pltpu.CompilerParams(vmem_limit_bytes=40 * 2**20),
+        cost_estimate=pl.CostEstimate(flops=a.size, bytes_accessed=4 * a.size, transcendentals=0),
+    )(a)
+
+
 def solution(mesh):
     rows = P(("dp", "tp"), None)
     both = P("dp", "tp")
@@ -283,11 +427,12 @@
     def body(x, dy, gate, up, w_gate, w_up, w_down):
         full, d_gate, d_up, hidden, dx = gather(mesh, x, dy, gate, up, w_gate, w_up, w_down)
         dx = lax.psum_scatter(dx, "tp", scatter_dimension=0, tiled=True)
+        full, dw_down = finish(mesh, full, hidden)
 
         def dw(a, b):
             return lax.dot_general(a, b, TN, preferred_element_type=F32).astype(BF16)
 
-        return dx, dw(full[1], d_gate), dw(full[1], d_up), dw(hidden, full[0])
+        return dx, dw(full[1], d_gate), dw(full[1], d_up), copied(dw_down)
 
     return jax.shard_map(
         body,

time: 553 us -> 547 us (0.989)
  matrix products: 179 us -> 120 us
  Pallas kernels: 348 us -> 401 us
    pallas_call x0 -> x2, Pallas kernels: none -> 84.5 us  [the longest x1 65.2 us: finish(): pl.pallas_call(functools.partial(late_kernel, n, tile_d), name='finish',...]
    dot_general x3 -> x2, matrix products: 179 us -> 120 us  [dw(): return lax.dot_general(a, b, TN, preferred_element_type=F32).astype(BF16)]
    pallas_call x1, Pallas kernels: 348 us -> 317 us  [gather(): pl.pallas_call(functools.partial(gather_kernel, n, tile_f, tile_d), name=...]
  transfers between devices with their start and end apart: 1 -> 1, of which waited for: 1 -> 1; matrix products, arithmetic and copies ran while one was open for 32% -> 22% of each run, Pallas kernels for 0% -> 15%
where the time goes in v2:
time: 547 us
  Pallas kernels  401 us (73%)
  matrix products  120 us (22%)
  between operations  14.1 us (3%)
  waiting for transfers between devices  11.3 us (2%)
    pallas_call x1, Pallas kernels, gather(): pl.pallas_call(functools.partial(gather_kernel, n, tile_f, tile_d), name=...  317 us
    dot_general x2, matrix products, dw(): return lax.dot_general(a, b, TN, preferred_element_type=F32).astype(BF16)  120 us
    pallas_call x1, Pallas kernels, finish(): pl.pallas_call(functools.partial(late_kernel, n, tile_d), name='finish',...  65.2 us
    pallas_call x1, Pallas kernels, copied(): pl.pallas_call(copy_kernel, name='copied', grid=(a.shape[0] // rows,), ou...  19.3 us
    reduce_scatter x1, waiting for transfers between devices, body(): dx = lax.psum_scatter(dx, 'tp', scatter_dimension=0, tiled=True)  11.2 us
  transfers between devices with their start and end apart: 1, of which 1 were waited for; matrix products, arithmetic and copies ran while one was open for 22% of the time, Pallas kernels for 15%

profile of v2, /device:TPU:97, one launch (start us, length us, event | category | flops | bytes accessed | tf_op | source)
XLA Modules:
  0.0 546.8 jit_solution(29098357953769593)
XLA Ops:
  7.2 0.1 reduce-scatter.2.cloned.1.call-start
  7.2 316.8 %gather.1 = (bf16[2,2048,8192]{2,1,0:T(8,128)(2,1)}, bf16[2048,1536]{1,0:T(8,128)(2,1)}, bf16[2048,1536]{1,0:T(8,128)(2,1)}, bf16[2048,1536]{1,0:T(8,128)(2,1)}, bf16[2048,8192]{1,0:T(8,128)(2,1)}) custom-call(bf16[128,8192]{1,0:T(8,128)(2,1)} %x_ref.1, bf16[128,8192]{1,0:T(8,128)(2,1)} %dy_ref.1, bf16[2048,1536]{1,0:T(8,128)(2,1)} %gate_ref.1, ...), custom_call_target="tpu_custom_call" | custom-call | flops 154618822656 | bytes 301989888 | tf_op jit(solution)/shard_map/gather/pallas_call | solution.py:280
  324.1 0.1 reduce-scatter.2.cloned.1.call-update
  324.1 65.2 %finish.1 = (bf16[2,2048,8192]{2,1,0:T(8,128)(2,1)}, bf16[1536,8192]{1,0:T(8,128)(2,1)}) custom-call(bf16[2,2048,8192]{2,1,0:T(8,128)(2,1)} %get-tuple-element.12.full_in_ref, bf16[2048,1536]{1,0:T(8,128)(2,1)} %get-tuple-element.13.hidden_ref), custom_call_target="tpu_custom_call", output_to_operand_aliasing={{0}: (0, {})} | custom-call | flops 51539607552 | bytes 65011712 | tf_op jit(solution)/shard_map/finish/pallas_call | solution.py:380
  389.3 0.0 copy-start
  389.3 0.0 slice-start
  389.3 19.3 %copied.1 = bf16[1536,8192]{1,0:T(8,128)(2,1)} custom-call(bf16[1536,8192]{1,0:T(8,128)(2,1)} %get-tuple-element.17.src_ref), custom_call_target="tpu_custom_call" | custom-call | flops 12582912 | bytes 50331648 | tf_op jit(solution)/shard_map/copied/pallas_call | solution.py:410
  408.6 0.0 copy-done
  408.6 0.0 slice-start.1
  408.6 60.0 %fusion.7 = bf16[8192,1536]{1,0:T(8,128)(2,1)} fusion(bf16[2048,1536]{1,0:T(8,128)(2,1)S(1)} %copy-done, bf16[2,2048,8192]{2,1,0:T(8,128)(2,1)} %get-tuple-element.14), kind=kOutput, calls=%fused_computation.5 | convolution fusion | flops 51552190464 | bytes 65011712 | tf_op jit(solution)/shard_map/dot_general | solution.py:433
  468.7 0.0 slice-done
  468.7 0.0 slice-done.1
  468.7 60.0 %fusion.4 = bf16[8192,1536]{1,0:T(8,128)(2,1)} fusion(bf16[2048,1536]{1,0:T(8,128)(2,1)S(1)} %bitcast.15, bf16[2,2048,8192]{2,1,0:T(8,128)(2,1)} %get-tuple-element.14), kind=kOutput, calls=%fused_computation.4 | convolution fusion | flops 51552190464 | bytes 65011712 | tf_op jit(solution)/shard_map/dot_general | solution.py:433
  528.7 11.2 %reduce-scatter.2.cloned.1.call-done = bf16[128,8192]{1,0:T(8,128)(2,1)} async-done(((bf16[2048,8192]{1,0:T(8,128)(2,1)}), bf16[128,8192]{1,0:T(8,128)(2,1)}) %reduce-scatter.2.cloned.1.call-update) | async-done | bytes 2097168 | tf_op jit(solution)/shard_map/reduce_scatter | solution.py:429
  (1 shorter events, 0.0 us)
Async XLA Ops:
  7.2 532.7 %reduce-scatter.2.cloned.1.call-start = ((), (), s32[]{:S(2)}) async-start(), calls=%async_computation.1 | async-start | bytes 35651584 | tf_op jit(solution)/shard_map/reduce_scatter | solution.py:429
  389.3 19.3 %copy-start = (bf16[2048,1536]{1,0:T(8,128)(2,1)S(1)}, bf16[2048,1536]{1,0:T(8,128)(2,1)}, u32[]{:S(2)}) copy-start(bf16[2048,1536]{1,0:T(8,128)(2,1)} %get-tuple-element.16) | copy-start | bytes 18874372
  389.3 79.4 %slice-start = ((s8[6291456]{0:T(1024)(128)(4,1)}), s8[4194304]{0:T(1024)(128)(4,1)S(1)}, s32[]{:S(2)}) async-start(s8[6291456]{0:T(1024)(128)(4,1)} %bitcast.14), calls=%async_computation.2 | async-start | bytes 8388608
  408.6 60.1 %slice-start.1 = ((s8[6291456]{0:T(1024)(128)(4,1)}), s8[2097152]{0:T(1024)(128)(4,1)S(1)}, s32[]{:S(2)}) async-start(s8[6291456]{0:T(1024)(128)(4,1)} %bitcast.14), calls=%async_computation.3 | async-start | bytes 4194304
Sparse Core Ops, SparseCore 0:
  324.2 215.6 reduce-scatter.1

commit v3 on v2

--- a/solution.py
+++ b/solution.py
@@ -10,9 +10,10 @@
 
 RINGS = 4
 SUBS = 4
-LATE = 3
+LATE = 2
 FETCH = 2
 TILE_A = 2
+TAIL = 8
 BF16 = jnp.bfloat16
 F32 = jnp.float32
 NT = (((1,), (1,)), ((), ()))
@@ -139,10 +140,11 @@
 
     units = FETCH + TILE_A * tiles_a + tiles_b
     first = (per_block - 1) * SUBS
+    paced = messages - TAIL
 
     def serve_between(block, since, until):
         def served(unit):
-            return first + (block * units + unit) * (messages - first) // (blocks * units)
+            return first + (block * units + unit) * (paced - first) // (blocks * units)
 
         lax.fori_loop(served(since), served(until), lambda i, c: serve(i), None)
 
@@ -265,7 +267,9 @@
         for i, ref in enumerate((dg_ref, du_ref, hid_ref)):
             pltpu.make_async_copy(grads.at[i], ref.at[pl.ds(0, blk.shape[0]), :], grads_sem.at[i]).wait()
 
+    assert all(first + b * (paced - first) // blocks >= ((b + 1) * per_block - 1) * SUBS for b in range(blocks))
     lax.fori_loop(0, blocks, one_block, None)
+    lax.fori_loop(paced, messages, lambda i, c: serve(i), None)
     ring.sent(messages)
 
 
@@ -327,22 +331,23 @@
     messages = LATE * SUBS
     first = stop - messages
 
-    load = pltpu.make_async_copy(hidden_ref, hid, hid_sem)
-    load.start()
-
-    def load_dy(j, slot):
-        at = pl.ds(pl.multiple_of(j * tile_d, tile_d), tile_d)
-        return pltpu.make_async_copy(full_ref.at[0, :, at], dy_buf.at[slot], dy_sem.at[slot])
-
-    def store(j, slot):
-        at = pl.ds(pl.multiple_of(j * tile_d, tile_d), tile_d)
-        return pltpu.make_async_copy(obuf.at[slot], dw_ref.at[:, at], o_sem.at[slot])
-
-    load_dy(0, 0).start()
     ring.greet()
     for sub in range(SUBS):
         for r in range(RINGS):
             ring.message(r, first // SUBS, sub, sub).start()
+
+    load = pltpu.make_async_copy(hidden_ref, hid, hid_sem)
+    load.start()
+
+    def load_dy(j, slot):
+        at = pl.ds(pl.multiple_of(j * tile_d, tile_d), tile_d)
+        return pltpu.make_async_copy(full_ref.at[0, :, at], dy_buf.at[slot], dy_sem.at[slot])
+
+    def store(j, slot):
+        at = pl.ds(pl.multiple_of(j * tile_d, tile_d), tile_d)
+        return pltpu.make_async_copy(obuf.at[slot], dw_ref.at[:, at], o_sem.at[slot])
+
+    load_dy(0, 0).start()
     load.wait()
 
     def tile(j, carry):
@@ -401,20 +406,54 @@
     )(full, hidden)
 
 
-def copy_kernel(src_ref, out_ref):
-    out_ref[...] = src_ref[...]
-
-
-def copied(a, rows=256):
-    spec = pl.BlockSpec((rows, a.shape[1]), lambda i: (i, 0))
+def copy_kernel(src_ref, out_ref, buf, in_sem, out_sem):
+    slots, rows, _ = buf.shape
+    ahead = slots // 2
+    chunks = src_ref.shape[0] // rows
+
+    def chunk(ref, i):
+        return ref.at[pl.ds(pl.multiple_of(i * rows, rows), rows), :]
+
+    def load(i):
+        return pltpu.make_async_copy(chunk(src_ref, i), buf.at[i % slots], in_sem.at[i % slots])
+
+    def store(i):
+        return pltpu.make_async_copy(buf.at[i % slots], chunk(out_ref, i), out_sem.at[i % slots])
+
+    for i in range(ahead):
+        load(i).start()
+
+    def step(i, carry):
+        load(i).wait()
+        store(i).start()
+
+        @pl.when(jnp.logical_and(i + ahead >= slots, i + ahead < chunks))
+        def _():
+            store(i + ahead - slots).wait()
+
+        @pl.when(i + ahead < chunks)
+        def _():
+            load(i + ahead).start()
+
+    lax.fori_loop(0, chunks, step, None)
+    for i in range(chunks - slots, chunks):
+        store(i).wait()
+
+
+def copied(a, rows=64, slots=8):
+    hbm = pl.BlockSpec(memory_space=pl.ANY)
     return pl.pallas_call(
         copy_kernel,
         name="copied",
-        grid=(a.shape[0] // rows,),
         out_shape=jax.ShapeDtypeStruct(a.shape, a.dtype),
-        in_specs=[spec],
-        out_specs=spec,
-        compiler_params=pltpu.CompilerParams(vmem_limit_bytes=40 * 2**20),
+        in_specs=[hbm],
+        out_specs=hbm,
+        scratch_shapes=[
+            pltpu.VMEM((slots, rows, a.shape[1]), a.dtype),
+            pltpu.SemaphoreType.DMA((slots,)),
+            pltpu.SemaphoreType.DMA((slots,)),
+        ],
+        compiler_params=pltpu.CompilerParams(vmem_limit_bytes=60 * 2**20),
         cost_estimate=pl.CostEstimate(flops=a.size, bytes_accessed=4 * a.size, transcendentals=0),
     )(a)
 

time: 547 us -> 546 us (level)
  Pallas kernels: 401 us -> 410 us
  waiting for transfers between devices: 11.3 us -> 2.62 us
    pallas_call x1, Pallas kernels: 317 us -> 327 us  [gather(): pl.pallas_call(functools.partial(gather_kernel, n, tile_f, tile_d), name=...]
    reduce_scatter x1, waiting for transfers between devices: 11.2 us -> 2.56 us  [body(): dx = lax.psum_scatter(dx, 'tp', scatter_dimension=0, tiled=True)]
where the time goes in v3:
time: 546 us
  Pallas kernels  410 us (75%)
  matrix products  119 us (22%)
  between operations  14.1 us (3%)
    pallas_call x1, Pallas kernels, gather(): pl.pallas_call(functools.partial(gather_kernel, n, tile_f, tile_d), name=...  327 us
    dot_general x2, matrix products, dw(): return lax.dot_general(a, b, TN, preferred_element_type=F32).astype(BF16)  119 us
    pallas_call x1, Pallas kernels, finish(): pl.pallas_call(functools.partial(late_kernel, n, tile_d), name='finish',...  65 us
    pallas_call x1, Pallas kernels, copied(): pl.pallas_call(copy_kernel, name='copied', out_shape=jax.ShapeDtypeStruct...  18 us
  transfers between devices with their start and end apart: 1, of which 1 were waited for; matrix products, arithmetic and copies ran while one was open for 22% of the time, Pallas kernels for 15%

profile of v3, /device:TPU:97, one launch (start us, length us, event | category | flops | bytes accessed | tf_op | source)
XLA Modules:
  0.0 545.9 jit_solution(10901344903638581815)
XLA Ops:
  7.2 0.1 reduce-scatter.2.cloned.1.call-start
  7.2 327.2 %gather.1 = (bf16[2,2048,8192]{2,1,0:T(8,128)(2,1)}, bf16[2048,1536]{1,0:T(8,128)(2,1)}, bf16[2048,1536]{1,0:T(8,128)(2,1)}, bf16[2048,1536]{1,0:T(8,128)(2,1)}, bf16[2048,8192]{1,0:T(8,128)(2,1)}) custom-call(bf16[128,8192]{1,0:T(8,128)(2,1)} %x_ref.1, bf16[128,8192]{1,0:T(8,128)(2,1)} %dy_ref.1, bf16[2048,1536]{1,0:T(8,128)(2,1)} %gate_ref.1, ...), custom_call_target="tpu_custom_call" | custom-call | flops 154618822656 | bytes 301989888 | tf_op jit(solution)/shard_map/gather/pallas_call | solution.py:284
  334.5 0.1 reduce-scatter.2.cloned.1.call-update
  334.6 65.0 %finish.1 = (bf16[2,2048,8192]{2,1,0:T(8,128)(2,1)}, bf16[1536,8192]{1,0:T(8,128)(2,1)}) custom-call(bf16[2,2048,8192]{2,1,0:T(8,128)(2,1)} %get-tuple-element.12.full_in_ref, bf16[2048,1536]{1,0:T(8,128)(2,1)} %get-tuple-element.13.hidden_ref), custom_call_target="tpu_custom_call", output_to_operand_aliasing={{0}: (0, {})} | custom-call | flops 51539607552 | bytes 65011712 | tf_op jit(solution)/shard_map/finish/pallas_call | solution.py:385
  399.6 0.0 slice-start
  399.6 18.0 %copied.1 = bf16[1536,8192]{1,0:T(8,128)(2,1)} custom-call(bf16[1536,8192]{1,0:T(8,128)(2,1)} %get-tuple-element.17.src_ref), custom_call_target="tpu_custom_call" | custom-call | flops 12582912 | bytes 50331648 | tf_op jit(solution)/shard_map/copied/pallas_call | solution.py:445
  417.6 0.0 slice-start.1
  417.6 60.4 %fusion.7 = bf16[8192,1536]{1,0:T(8,128)(2,1)} fusion(bf16[2048,1536]{1,0:T(8,128)(2,1)} %get-tuple-element.16, bf16[2,2048,8192]{2,1,0:T(8,128)(2,1)} %get-tuple-element.14), kind=kOutput, calls=%fused_computation.5 | convolution fusion | flops 51552190464 | bytes 65011712 | tf_op jit(solution)/shard_map/dot_general | solution.py:472
  478.1 0.0 slice-done
  478.1 0.0 slice-done.1
  478.1 58.4 %fusion.4 = bf16[8192,1536]{1,0:T(8,128)(2,1)} fusion(bf16[2048,1536]{1,0:T(8,128)(2,1)S(1)} %bitcast.15, bf16[2,2048,8192]{2,1,0:T(8,128)(2,1)} %get-tuple-element.14), kind=kOutput, calls=%fused_computation.4 | convolution fusion | flops 51552190464 | bytes 65011712 | tf_op jit(solution)/shard_map/dot_general | solution.py:472
  536.5 2.6 reduce-scatter.2.cloned.1.call-done
  (1 shorter events, 0.0 us)
Async XLA Ops:
  7.2 531.9 %reduce-scatter.2.cloned.1.call-start = ((), (), s32[]{:S(2)}) async-start(), calls=%async_computation.1 | async-start | bytes 35651584 | tf_op jit(solution)/shard_map/reduce_scatter | solution.py:468
  399.6 78.5 %slice-start = ((s8[6291456]{0:T(1024)(128)(4,1)}), s8[2097152]{0:T(1024)(128)(4,1)S(1)}, s32[]{:S(2)}) async-start(s8[6291456]{0:T(1024)(128)(4,1)} %bitcast.14), calls=%async_computation.2 | async-start | bytes 4194304
  417.6 60.4 %slice-start.1 = ((s8[6291456]{0:T(1024)(128)(4,1)}), s8[4194304]{0:T(1024)(128)(4,1)S(1)}, s32[]{:S(2)}) async-start(s8[6291456]{0:T(1024)(128)(4,1)} %bitcast.14), calls=%async_computation.3 | async-start | bytes 8388608
Sparse Core Ops, SparseCore 0:
  334.7 204.3 reduce-scatter.1

commit v4 on v3

--- a/solution.py
+++ b/solution.py
@@ -10,10 +10,11 @@
 
 RINGS = 4
 SUBS = 4
-LATE = 2
+LATE = 3
 FETCH = 2
 TILE_A = 2
 TAIL = 8
+GROUP = 4
 BF16 = jnp.bfloat16
 F32 = jnp.float32
 NT = (((1,), (1,)), ((), ()))
@@ -100,7 +101,7 @@
     n, tile_f, tile_d,
     x_ref, dy_ref, gate_ref, up_ref, wg_ref, wu_ref, wd_ref,
     full_ref, dg_ref, du_ref, hid_ref, dx_ref,
-    blk, wd_buf, w2_buf, gu_buf, dh_buf, grads, obuf,
+    blk, wd_buf, w2_buf, gu_buf, dh_buf, grads,
     send_sem, recv_sem, blk_sem, wd_sem, w2_sem, gu_sem, grads_sem, o_sem,
 ):
     side = math.isqrt(n)
@@ -210,7 +211,7 @@
                 grads[1, at, cols] = dup.astype(BF16)
                 grads[2, at, cols] = h.astype(BF16)
 
-            lax.fori_loop(0, blk.shape[0] // chunk, elementwise, None)
+            lax.fori_loop(0, blk.shape[0] // chunk, elementwise, None, unroll=4)
             serve_between(block, FETCH + TILE_A * j, FETCH + TILE_A * (j + 1))
 
         lax.fori_loop(0, tiles_a, tile_a_body, None)
@@ -227,11 +228,6 @@
         def _():
             load_wd(0, 0).start()
 
-        def wait_out(slot):
-            pltpu.make_async_copy(
-                obuf.at[slot], dx_ref.at[pl.ds(0, blk.shape[0]), pl.ds(0, tile_d)], o_sem.at[slot]
-            ).wait()
-
         def tile_b_body(j, carry):
             slot = j % 2
             for c in load_w2(j, slot):
@@ -242,28 +238,28 @@
                 for c in load_w2(j + 1, 1 - slot):
                     c.start()
 
-            @pl.when(j >= 2)
-            def _():
-                wait_out(slot)
-
-            obuf[slot] = (
+            blk[:, pl.ds(pl.multiple_of(j * tile_d, tile_d), tile_d)] = (
                 lax.dot_general(grads[0], w2_buf[slot, 0], NT, preferred_element_type=F32)
                 + lax.dot_general(grads[1], w2_buf[slot, 1], NT, preferred_element_type=F32)
             ).astype(BF16)
-            cols = pl.ds(pl.multiple_of(j * tile_d, tile_d), tile_d)
-
-            def put(there, here):
-                pltpu.make_async_copy(
-                    obuf.at[slot, pl.ds(here, piece), :], dx_ref.at[pl.ds(there, piece), cols], o_sem.at[slot]
-                ).start()
-
-            pieces(block, put)
+
+            @pl.when(j % GROUP == GROUP - 1)
+            def _():
+                width = GROUP * tile_d
+                cols = pl.ds(pl.multiple_of(j // GROUP * width, width), width)
+
+                def put(there, here):
+                    pltpu.make_async_copy(
+                        blk.at[pl.ds(here, piece), cols], dx_ref.at[pl.ds(there, piece), cols], o_sem
+                    ).start()
+
+                pieces(block, put)
+
             done = FETCH + TILE_A * tiles_a + j
             serve_between(block, done, done + 1)
 
         lax.fori_loop(0, tiles_b, tile_b_body, None)
-        for slot in range(2):
-            wait_out(slot)
+        pltpu.make_async_copy(blk, dx_ref.at[pl.ds(0, blk.shape[0]), :], o_sem).wait()
         for i, ref in enumerate((dg_ref, du_ref, hid_ref)):
             pltpu.make_async_copy(grads.at[i], ref.at[pl.ds(0, blk.shape[0]), :], grads_sem.at[i]).wait()
 
@@ -298,7 +294,6 @@
             pltpu.VMEM((2, block, ff), BF16),
             pltpu.VMEM((block, tile_f), F32),
             pltpu.VMEM((3, block, ff), BF16),
-            pltpu.VMEM((2, block, tile_d), BF16),
             pltpu.SemaphoreType.DMA,
             pltpu.SemaphoreType.DMA((RINGS, messages)),
             pltpu.SemaphoreType.DMA,
@@ -306,7 +301,7 @@
             pltpu.SemaphoreType.DMA((2, 2)),
             pltpu.SemaphoreType.DMA((2,)),
             pltpu.SemaphoreType.DMA((3,)),
-            pltpu.SemaphoreType.DMA((2,)),
+            pltpu.SemaphoreType.DMA,
         ],
         compiler_params=pltpu.CompilerParams(collective_id=0, has_side_effects=True, vmem_limit_bytes=58 * 2**20),
         cost_estimate=pl.CostEstimate(
@@ -377,7 +372,7 @@
     ring.sent(messages)
 
 
-def finish(mesh, full, hidden, tile_d=256):
+def finish(mesh, full, hidden, tile_d=512):
     n = mesh.shape["tp"]
     _, total, d_model = full.shape
     ff = hidden.shape[1]

time: 546 us -> 546 us (level)
  waiting for transfers between devices: 2.62 us -> 16.2 us
  Pallas kernels: 410 us -> 397 us
    reduce_scatter x1, waiting for transfers between devices: 2.56 us -> 16.1 us  [body(): dx = lax.psum_scatter(dx, 'tp', scatter_dimension=0, tiled=True)]
    pallas_call x1, Pallas kernels: 327 us -> 316 us  [gather(): pl.pallas_call(functools.partial(gather_kernel, n, tile_f, tile_d), name=...]
where the time goes in v4:
time: 546 us
  Pallas kernels  397 us (73%)
  matrix products  119 us (22%)
  waiting for transfers between devices  16.2 us (3%)
  between operations  14.1 us (3%)
    pallas_call x1, Pallas kernels, gather(): pl.pallas_call(functools.partial(gather_kernel, n, tile_f, tile_d), name=...  316 us
    dot_general x2, matrix products, dw(): return lax.dot_general(a, b, TN, preferred_element_type=F32).astype(BF16)  119 us
    pallas_call x1, Pallas kernels, finish(): pl.pallas_call(functools.partial(late_kernel, n, tile_d), name='finish',...  62.7 us
    pallas_call x1, Pallas kernels, copied(): pl.pallas_call(copy_kernel, name='copied', out_shape=jax.ShapeDtypeStruct...  18 us
    reduce_scatter x1, waiting for transfers between devices, body(): dx = lax.psum_scatter(dx, 'tp', scatter_dimension=0, tiled=True)  16.1 us
  transfers between devices with their start and end apart: 1, of which 1 were waited for; matrix products, arithmetic and copies ran while one was open for 22% of the time, Pallas kernels for 15%

profile of v4, /device:TPU:97, one launch (start us, length us, event | category | flops | bytes accessed | tf_op | source)
XLA Modules:
  0.0 545.9 jit_solution(4742745408847511203)
XLA Ops:
  7.2 0.1 reduce-scatter.2.cloned.1.call-start
  7.2 315.9 %gather.1 = (bf16[2,2048,8192]{2,1,0:T(8,128)(2,1)}, bf16[2048,1536]{1,0:T(8,128)(2,1)}, bf16[2048,1536]{1,0:T(8,128)(2,1)}, bf16[2048,1536]{1,0:T(8,128)(2,1)}, bf16[2048,8192]{1,0:T(8,128)(2,1)}) custom-call(bf16[128,8192]{1,0:T(8,128)(2,1)} %x_ref.1, bf16[128,8192]{1,0:T(8,128)(2,1)} %dy_ref.1, bf16[2048,1536]{1,0:T(8,128)(2,1)} %gate_ref.1, ...), custom_call_target="tpu_custom_call" | custom-call | flops 154618822656 | bytes 301989888 | tf_op jit(solution)/shard_map/gather/pallas_call | solution.py:280
  323.2 0.1 reduce-scatter.2.cloned.1.call-update
  323.2 62.7 %finish.1 = (bf16[2,2048,8192]{2,1,0:T(8,128)(2,1)}, bf16[1536,8192]{1,0:T(8,128)(2,1)}) custom-call(bf16[2,2048,8192]{2,1,0:T(8,128)(2,1)} %get-tuple-element.12.full_in_ref, bf16[2048,1536]{1,0:T(8,128)(2,1)} %get-tuple-element.13.hidden_ref), custom_call_target="tpu_custom_call", output_to_operand_aliasing={{0}: (0, {})} | custom-call | flops 51539607552 | bytes 65011712 | tf_op jit(solution)/shard_map/finish/pallas_call | solution.py:380
  385.9 0.0 slice-start
  386.0 18.0 %copied.1 = bf16[1536,8192]{1,0:T(8,128)(2,1)} custom-call(bf16[1536,8192]{1,0:T(8,128)(2,1)} %get-tuple-element.17.src_ref), custom_call_target="tpu_custom_call" | custom-call | flops 12582912 | bytes 50331648 | tf_op jit(solution)/shard_map/copied/pallas_call | solution.py:440
  404.0 0.0 slice-start.1
  404.0 60.4 %fusion.7 = bf16[8192,1536]{1,0:T(8,128)(2,1)} fusion(bf16[2048,1536]{1,0:T(8,128)(2,1)} %get-tuple-element.16, bf16[2,2048,8192]{2,1,0:T(8,128)(2,1)} %get-tuple-element.14), kind=kOutput, calls=%fused_computation.5 | convolution fusion | flops 51552190464 | bytes 65011712 | tf_op jit(solution)/shard_map/dot_general | solution.py:467
  464.4 0.0 slice-done
  464.4 0.0 slice-done.1
  464.4 58.4 %fusion.4 = bf16[8192,1536]{1,0:T(8,128)(2,1)} fusion(bf16[2048,1536]{1,0:T(8,128)(2,1)S(1)} %bitcast.15, bf16[2,2048,8192]{2,1,0:T(8,128)(2,1)} %get-tuple-element.14), kind=kOutput, calls=%fused_computation.4 | convolution fusion | flops 51552190464 | bytes 65011712 | tf_op jit(solution)/shard_map/dot_general | solution.py:467
  522.9 16.1 %reduce-scatter.2.cloned.1.call-done = bf16[128,8192]{1,0:T(8,128)(2,1)} async-done(((bf16[2048,8192]{1,0:T(8,128)(2,1)}), bf16[128,8192]{1,0:T(8,128)(2,1)}) %reduce-scatter.2.cloned.1.call-update) | async-done | bytes 2097168 | tf_op jit(solution)/shard_map/reduce_scatter | solution.py:463
  (1 shorter events, 0.0 us)
Async XLA Ops:
  7.2 531.8 %reduce-scatter.2.cloned.1.call-start = ((), (), s32[]{:S(2)}) async-start(), calls=%async_computation.1 | async-start | bytes 35651584 | tf_op jit(solution)/shard_map/reduce_scatter | solution.py:463
  385.9 78.5 %slice-start = ((s8[6291456]{0:T(1024)(128)(4,1)}), s8[2097152]{0:T(1024)(128)(4,1)S(1)}, s32[]{:S(2)}) async-start(s8[6291456]{0:T(1024)(128)(4,1)} %bitcast.14), calls=%async_computation.2 | async-start | bytes 4194304
  404.0 60.4 %slice-start.1 = ((s8[6291456]{0:T(1024)(128)(4,1)}), s8[4194304]{0:T(1024)(128)(4,1)S(1)}, s32[]{:S(2)}) async-start(s8[6291456]{0:T(1024)(128)(4,1)} %bitcast.14), calls=%async_computation.3 | async-start | bytes 8388608
Sparse Core Ops, SparseCore 0:
  323.4 215.6 reduce-scatter.1
